TPU v7x, 32 devices: a whole 2x2x4 slice. The times are simulated.
32 devices in a mesh: groups: 2 (over y), ctx: 4 (over z), head: 2 (over x), rep: 2 (over core).
Axes of the slice: x: 2, y: 2, z: 4, core: 2. Of those that a mesh axis runs over, the one named last changes fastest.
Arguments:
- queries: bfloat16 [2048, 4096], P(('groups', 'ctx'), ('head', 'rep')), parts along dimension 0, may hold values from -24 to 24
- keys: bfloat16 [2048, 1024], P(('groups', 'ctx'), ('head', 'rep')), parts along dimension 0, may hold values from -6 to 6
- values: bfloat16 [2048, 1024], P(('groups', 'ctx'), ('head', 'rep')), parts along dimension 0, may hold values from -6 to 6
- span_order: int32 [8], replicated, may hold values from 0 to 7, as said below
Outputs:
- attended: bfloat16 [2048, 4096], P(('groups', 'ctx'), ('head', 'rep')), parts along dimension 0
There are 2 independent parts, one for each index of `groups`. A program takes and returns all parts, laid end to end along the dimension named above; an argument that names none is the same for every part. Nothing has to cross between parts.
Inputs may be any that keep to these rules, and one draw needn't show every extreme that they name: `span_order`: A permutation of the spans in which entries 2 d and 2 d + 1 are c and 7 - c for some c.
All inputs are finite; a program needn't handle non-finite values.
Results may differ from a plain program's by a relative error of at most 0.0047.
Values may be sent and summed in bfloat16 or wider, within the bound.
No kernel may reach another device: no remote copies, remote signals or barrier semaphores. Data moves between devices by JAX's collectives and lax.ppermute only.
A program may use at most 64 MiB of HBM per device.

v0:
```python
import math

import jax
import jax.numpy as jnp
from jax import lax
from jax.sharding import PartitionSpec as P

HEAD_SIZE = 128


masked_score = -1e30


def lookup_positions(span_order, first_row, row_count, span_rows):
    row_ids = first_row + jnp.arange(row_count, dtype=jnp.int32)
    span_ids = row_ids // span_rows
    span_table = jnp.arange(span_order.shape[0], dtype=jnp.int32)
    span_starts = jnp.sum(
        jnp.where(span_ids[:, None] == span_table[None, :], span_order[None, :], 0), axis=1
    )
    return span_starts * span_rows + row_ids % span_rows


def source_partials(query_block, query_pos, key_group, value_group, key_pos, head_dim):
    score_scale = 1.0 / math.sqrt(head_dim)
    scores = (
        jnp.einsum("rhgd,cshd->crhgs", query_block, key_group, preferred_element_type=jnp.float32)
        * score_scale
    )
    allowed = (key_pos[:, None, :] <= query_pos[None, :, None])[:, :, None, None, :]
    masked = jnp.where(allowed, scores, masked_score)
    row_top = jnp.max(masked, axis=-1)
    weights = jnp.where(allowed, jnp.exp(masked - row_top[..., None]), 0.0)
    row_total = jnp.sum(weights, axis=-1)
    numerator = jnp.einsum(
        "crhgs,cshd->crhgd",
        weights.astype(jnp.bfloat16),
        value_group,
        preferred_element_type=jnp.float32,
    )
    partial_value = (numerator / jnp.maximum(row_total, 1.0)[..., None]).astype(jnp.bfloat16)
    return (partial_value, row_top, row_total)


def absorb(running, partial_value, row_top, row_total):
    run_top, run_total, run_sum = running
    new_top = jnp.maximum(run_top, row_top)
    rescale = jnp.exp(run_top - new_top)
    source_weight = row_total * jnp.exp(row_top - new_top)
    return (
        new_top,
        run_total * rescale + source_weight,
        run_sum * rescale[..., None] + source_weight[..., None] * partial_value.astype(jnp.float32),
    )


def shards(queries, keys, values, span_order):
    rows_here = queries.shape[0]
    span_rows = rows_here // 2
    head_dim = HEAD_SIZE
    kv_heads = keys.shape[1] // head_dim
    common_values = queries.shape[1] // keys.shape[1]
    my_index = lax.axis_index("ctx")
    own_pos = lookup_positions(span_order, my_index * rows_here, rows_here, span_rows)
    q_local = queries.reshape(rows_here, kv_heads, common_values, head_dim)
    initial = (
        jnp.full((rows_here, kv_heads, common_values), masked_score, jnp.float32),
        jnp.zeros((rows_here, kv_heads, common_values), jnp.float32),
        jnp.zeros((rows_here, kv_heads, common_values, head_dim), jnp.float32),
    )
    running = initial
    k_piece = lax.all_gather(keys, "ctx", axis=0, tiled=True)
    v_piece = lax.all_gather(values, "ctx", axis=0, tiled=True)
    shard_count = k_piece.shape[0] // rows_here
    per_turn = 2
    turn_count = shard_count // per_turn
    k_pos = lookup_positions(span_order, jnp.int32(0), k_piece.shape[0], span_rows)
    k_steps = k_piece.reshape(turn_count, per_turn, rows_here, kv_heads, head_dim)
    v_steps = v_piece.reshape(turn_count, per_turn, rows_here, kv_heads, head_dim)
    p_steps = k_pos.reshape(turn_count, per_turn, rows_here)

    def one_turn(carried, inputs_now):
        partial_value, row_top, row_total = source_partials(
            q_local, own_pos, inputs_now[0], inputs_now[1], inputs_now[2], head_dim
        )
        for member in range(per_turn):
            carried = absorb(carried, partial_value[member], row_top[member], row_total[member])
        return (carried, None)

    running, unused = lax.scan(one_turn, running, (k_steps, v_steps, p_steps))
    merged = running[2] / running[1][..., None]
    return merged.reshape(rows_here, kv_heads * common_values * head_dim).astype(jnp.bfloat16)


def solution(mesh):
    return jax.shard_map(
        shards,
        mesh=mesh,
        in_specs=(
            P(("groups", "ctx"), ("head", "rep")),
            P(("groups", "ctx"), ("head", "rep")),
            P(("groups", "ctx"), ("head", "rep")),
            P(),
        ),
        out_specs=P(("groups", "ctx"), ("head", "rep")),
        check_vma=False,
    )
```

profile of v0, /device:TPU:0, one launch (start us, length us, event | category | flops | bytes accessed | tf_op | source)
XLA Modules:
  0.0 60.6 jit_solution(10825627206917604020)
XLA Ops:
  0.0 0.0 copy-start
  0.0 0.8 %select_reduce_fusion.1 = s32[256]{0:T(256)S(1)} fusion(s32[8]{0:T(128)} %param.9, s32[256]{0:T(256)S(1)} %and_select_fusion.2), kind=kLoop, calls=%fused_computation.45 | loop fusion | flops 5888 | bytes 2080 | tf_op jit(solution)/shard_map/reduce_sum | solution.py:18
  0.8 1.2 %copy.30 = bf16[256,1024]{0,1:T(8,128)(2,1)S(1)} copy(bf16[256,1024]{1,0:T(8,128)(2,1)} %param.6) | data formatting | bytes 1048576 | tf_op args[0]
  2.1 1.0 %copy.32 = bf16[256,2,4,128]{3,0,2,1:T(8,128)(2,1)} copy(bf16[256,2,4,128]{0,3,2,1:T(8,128)(2,1)S(1)} %bitcast.99) | data formatting | bytes 1048576
  3.1 17.6 %all_gather.6 = bf16[1024,256]{1,0:T(8,128)(2,1)S(1)} all-gather(bf16[256,256]{1,0:T(8,128)(2,1)} %param.7), channel_id=1, replica_groups=mesh['groups'=2,'ctx'=4,'head'=2,'rep'=2] {'ctx'}, dimensions={0}, use_global_device_ids=true | all-gather | bytes 655360 | tf_op jit(solution)/shard_map/all_gather | solution.py:72
  20.7 0.9 %reshape.66 = bf16[2,2,256,2,128]{4,3,2,1,0:T(2,128)(2,1)} reshape(bf16[1024,256]{1,0:T(8,128)(2,1)S(1)} %all_gather.6) | data formatting | bytes 1048576 | tf_op jit(solution)/shard_map/reshape | solution.py:78
  21.6 16.6 %all_gather.7 = bf16[1024,256]{1,0:T(8,128)(2,1)S(1)} all-gather(bf16[256,256]{1,0:T(8,128)(2,1)} %param.8), channel_id=1, replica_groups=mesh['groups'=2,'ctx'=4,'head'=2,'rep'=2] {'ctx'}, dimensions={0}, use_global_device_ids=true | all-gather | bytes 655360 | tf_op jit(solution)/shard_map/all_gather | solution.py:73
  38.2 0.9 %reshape.68 = bf16[2,2,256,2,128]{4,3,2,1,0:T(2,128)(2,1)} reshape(bf16[1024,256]{1,0:T(8,128)(2,1)S(1)} %all_gather.7) | data formatting | bytes 1048576 | tf_op jit(solution)/shard_map/reshape | solution.py:79
  39.1 0.0 copy-done
  39.1 0.1 select_reduce_fusion
  39.3 20.2 %while.15 = (s32[]{:T(128)}, f32[256,2,4]{0,2,1:T(4,128)S(1)}, f32[256,2,4]{0,2,1:T(4,128)S(1)}, f32[256,2,4,128]{0,3,2,1:T(8,128)S(1)}, s32[2,2,256]{2,1,0:T(2,...) while((s32[]{:T(128)}, f32[256,2,4]{0,2,1:T(4,128)S(1)}, ...), condition=%wide.region_5.6_spmd.clone, body=%wide.region_2.5_spmd.clone.sunk | while | flops 549871616 | bytes 19995776 | solution.py:90
  39.3 1.4 %constant_dynamic-slice_fusion.3 = (bf16[1,2,256,2,128]{4,3,2,1,0:T(2,128)(2,1)S(1)}, bf16[1,2,256,2,128]{4,3,2,1,0:T(2,128)(2,1)S(1)}) fusion(bf16[2,2,256,2,128]{4,3,2,1,0:T(2,128)(2,1)} %get-tuple-element.251, s32[]{:T(128)} %get-tuple-element.232, bf16[2,2,256,2,128]{4,3,2,1,0:T(2,128)(2,1)} %get-tuple-element.249), kind=kLoop, calls=%fused_computation.38.clone.1 | loop fusion | bytes 1048580 | tf_op jit(solution)/shard_map/while/body/jit(dynamic_index_in_dim)/dynamic_slice | solution.py:90
  40.7 0.1 broadcast_compare_fusion.3
  40.8 1.9 %fusion.43 = (f32[2,256,2,4]{1,3,0,2:T(4,128)S(1)}, f32[2,2,256,256,4]{3,2,4,1,0:T(8,128)S(1)}) fusion(pred[2,256,256]{1,2,0:T(8,128)(4,1)S(1)} %broadcast_compare_fusion.3, bf16[256,2,4,128]{3,0,2,1:T(8,128)(2,1)} %get-tuple-element.250, bf16[1,2,256,2,128]{4,3,2,1,0:T(2,128)(2,1)S(1)} %get-tuple-element.209), kind=kOutput, calls=%fused_computation.2.clone.1 | convolution fusion | flops 271577088 | bytes 5128192 | tf_op jit(solution)/shard_map/while/body/eval_jaxpr/rhgd,cshd->crhgs/dot_general | solution.py:27
  42.7 1.2 %fusion.44 = (bf16[2,256,2,4,256]{1,4,3,0,2:T(8,128)(2,1)S(1)}, f32[2,256,2,4]{1,3,0,2:T(4,128)S(1)}) fusion(f32[2,2,256,256,4]{3,2,4,1,0:T(8,128)S(1)} %get-tuple-element.211, f32[2,256,2,4]{1,3,0,2:T(4,128)S(1)} %get-tuple-element.210, pred[2,256,256]{1,2,0:T(8,128)(4,1)S(1)} %broadcast_compare_fusion.3), kind=kLoop, calls=%fused_computation.3.clone.1 | loop fusion | flops 6287360 | bytes 6455296 | tf_op jit(solution)/shard_map/while/body/eval_jaxpr/convert_element_type | solution.py:37
  43.9 0.9 %copy.63 = bf16[1,2,256,2,128]{2,4,3,1,0:T(8,128)(2,1)} copy(bf16[1,2,256,2,128]{4,3,2,1,0:T(2,128)(2,1)S(1)} %get-tuple-element.216) | data formatting | bytes 524288 | tf_op jit(solution)/shard_map/while/body/jit(dynamic_index_in_dim)/dynamic_slice | solution.py:90
  44.8 2.4 %fusion.46 = bf16[2,256,2,4,128]{1,4,3,2,0:T(8,128)(2,1)} fusion(bf16[2,256,2,4,256]{1,4,3,0,2:T(8,128)(2,1)S(1)} %get-tuple-element.215, bf16[1,2,256,2,128]{2,4,3,1,0:T(8,128)(2,1)} %copy.63, f32[2,256,2,4]{1,3,0,2:T(4,128)S(1)} %get-tuple-element.212), kind=kOutput, calls=%fused_computation.6.clone.1 | convolution fusion | flops 269488128 | bytes 3424256 | tf_op jit(solution)/shard_map/while/body/eval_jaxpr/crhgs,cshd->crhgd/dot_general | solution.py:35
  47.2 2.1 %fusion.47 = f32[256,2,4,128]{0,3,2,1:T(8,128)S(1)} fusion(f32[256,2,4,128]{0,3,2,1:T(8,128)S(1)} %get-tuple-element.235, bf16[2,256,2,4,128]{1,4,3,2,0:T(8,128)(2,1)} %fusion.46, f32[256,2,4]{0,2,1:T(4,128)S(1)} %get-tuple-element.217, f32[256,2,4]{0,2,1:T(4,128)S(1)} %get-tuple-element.218, f32[256,2,4]{0,2,1:T(4,128)S(1)} %get-tuple-element.219, ...), kind=kLoop, calls=%fused_computation.10.clone.1 | loop fusion | flops 2359296 | bytes 3178497 | tf_op jit(solution)/shard_map/while/body/eval_jaxpr/add | solution.py:53
  49.4 1.4 %constant_dynamic-slice_fusion.3 = (bf16[1,2,256,2,128]{4,3,2,1,0:T(2,128)(2,1)S(1)}, bf16[1,2,256,2,128]{4,3,2,1,0:T(2,128)(2,1)S(1)}) fusion(bf16[2,2,256,2,128]{4,3,2,1,0:T(2,128)(2,1)} %get-tuple-element.251, s32[]{:T(128)} %get-tuple-element.232, bf16[2,2,256,2,128]{4,3,2,1,0:T(2,128)(2,1)} %get-tuple-element.249), kind=kLoop, calls=%fused_computation.38.clone.1 | loop fusion | bytes 1048580 | tf_op jit(solution)/shard_map/while/body/jit(dynamic_index_in_dim)/dynamic_slice | solution.py:90
  50.8 0.1 broadcast_compare_fusion.3
  50.9 1.9 %fusion.43 = (f32[2,256,2,4]{1,3,0,2:T(4,128)S(1)}, f32[2,2,256,256,4]{3,2,4,1,0:T(8,128)S(1)}) fusion(pred[2,256,256]{1,2,0:T(8,128)(4,1)S(1)} %broadcast_compare_fusion.3, bf16[256,2,4,128]{3,0,2,1:T(8,128)(2,1)} %get-tuple-element.250, bf16[1,2,256,2,128]{4,3,2,1,0:T(2,128)(2,1)S(1)} %get-tuple-element.209), kind=kOutput, calls=%fused_computation.2.clone.1 | convolution fusion | flops 271577088 | bytes 5128192 | tf_op jit(solution)/shard_map/while/body/eval_jaxpr/rhgd,cshd->crhgs/dot_general | solution.py:27
  52.8 1.2 %fusion.44 = (bf16[2,256,2,4,256]{1,4,3,0,2:T(8,128)(2,1)S(1)}, f32[2,256,2,4]{1,3,0,2:T(4,128)S(1)}) fusion(f32[2,2,256,256,4]{3,2,4,1,0:T(8,128)S(1)} %get-tuple-element.211, f32[2,256,2,4]{1,3,0,2:T(4,128)S(1)} %get-tuple-element.210, pred[2,256,256]{1,2,0:T(8,128)(4,1)S(1)} %broadcast_compare_fusion.3), kind=kLoop, calls=%fused_computation.3.clone.1 | loop fusion | flops 6287360 | bytes 6455296 | tf_op jit(solution)/shard_map/while/body/eval_jaxpr/convert_element_type | solution.py:37
  54.0 0.9 %copy.63 = bf16[1,2,256,2,128]{2,4,3,1,0:T(8,128)(2,1)} copy(bf16[1,2,256,2,128]{4,3,2,1,0:T(2,128)(2,1)S(1)} %get-tuple-element.216) | data formatting | bytes 524288 | tf_op jit(solution)/shard_map/while/body/jit(dynamic_index_in_dim)/dynamic_slice | solution.py:90
  54.9 2.4 %fusion.46 = bf16[2,256,2,4,128]{1,4,3,2,0:T(8,128)(2,1)} fusion(bf16[2,256,2,4,256]{1,4,3,0,2:T(8,128)(2,1)S(1)} %get-tuple-element.215, bf16[1,2,256,2,128]{2,4,3,1,0:T(8,128)(2,1)} %copy.63, f32[2,256,2,4]{1,3,0,2:T(4,128)S(1)} %get-tuple-element.212), kind=kOutput, calls=%fused_computation.6.clone.1 | convolution fusion | flops 269488128 | bytes 3424256 | tf_op jit(solution)/shard_map/while/body/eval_jaxpr/crhgs,cshd->crhgd/dot_general | solution.py:35
  57.3 2.1 %fusion.47 = f32[256,2,4,128]{0,3,2,1:T(8,128)S(1)} fusion(f32[256,2,4,128]{0,3,2,1:T(8,128)S(1)} %get-tuple-element.235, bf16[2,256,2,4,128]{1,4,3,2,0:T(8,128)(2,1)} %fusion.46, f32[256,2,4]{0,2,1:T(4,128)S(1)} %get-tuple-element.217, f32[256,2,4]{0,2,1:T(4,128)S(1)} %get-tuple-element.218, f32[256,2,4]{0,2,1:T(4,128)S(1)} %get-tuple-element.219, ...), kind=kLoop, calls=%fused_computation.10.clone.1 | loop fusion | flops 2359296 | bytes 3178497 | tf_op jit(solution)/shard_map/while/body/eval_jaxpr/add | solution.py:53
  59.5 0.1 divide_convert_fusion
  59.6 1.0 %copy.39 = bf16[256,1024]{1,0:T(8,128)(2,1)} copy(bf16[256,1024]{0,1:T(8,128)(2,1)S(1)} %bitcast.98) | data formatting | bytes 1048576 | tf_op jit(solution)/shard_map/convert_element_type | solution.py:92
  (13 shorter events, 0.1 us)
Async XLA Ops:
  0.0 39.1 %copy-start = (s32[8]{0:T(128)S(1)}, s32[8]{0:T(128)}, u32[]{:S(2)}) copy-start(s32[8]{0:T(128)} %param.9) | copy-start | bytes 100
where the time goes:
time: 61 us; the launch traced here: 60.6 us
  blocking collectives  34.1 us (56%)
  local copies, waits for them, and re-layouts  9.69 us (16%)
  matrix products  8.65 us (14%)
  other arithmetic  7.94 us (13%)
    all_gather x1, blocking collectives, shards(): k_piece = lax.all_gather(keys, 'ctx', axis=0, tiled=True)  17.6 us
    all_gather x1, blocking collectives, shards(): v_piece = lax.all_gather(values, 'ctx', axis=0, tiled=True)  16.6 us
    dot_general x2, matrix products, source_partials(): jnp.einsum('crhgs,cshd->crhgd', weights.astype(jnp.bfloat16), value_group...  4.85 us
    dynamic_slice x4, local copies, waits for them, and re-layouts, shards(): running, unused = lax.scan(one_turn, running, (k_steps, v_steps, p_steps))  4.53 us
    add x2, other arithmetic, absorb(): run_sum * rescale[..., None]  4.23 us
    dot_general x2, matrix products, source_partials(): jnp.einsum('rhgd,cshd->crhgs', query_block, key_group, preferred_element_...  3.8 us
    convert_element_type x2, other arithmetic, source_partials(): weights.astype(jnp.bfloat16)  2.34 us
    unnamed x4, local copies, waits for them, and re-layouts  2.27 us

commit v1 on v0

v1 whole, which is shorter than its diff:
```python
import math

import jax
import jax.numpy as jnp
from jax import lax
from jax.experimental import pallas as pl
from jax.experimental.pallas import tpu as pltpu
from jax.sharding import PartitionSpec as P

HEAD_SIZE = 128
LOW = -1e29
MASKED = -1e30


def attend_kernel(span_rows, group, plan, has_state, last, *refs):
    span_order, q_ref = refs[:2]
    at = 2
    pieces = []
    for _ in plan:
        pieces.append((refs[at], refs[at + 1]))
        at += 2
    if has_state:
        acc_in, stat_in = refs[at : at + 2]
        at += 2
    outs = refs[at:]
    rows = q_ref.shape[0]
    heads = q_ref.shape[1] // HEAD_SIZE
    me = lax.axis_index("ctx")
    factor = math.log2(math.e) / math.sqrt(HEAD_SIZE)

    def span_pos(source, shape, axis):
        ids = lax.broadcasted_iota(jnp.int32, shape, axis)
        first = span_order[2 * source] * span_rows
        second = (span_order[2 * source + 1] - 1) * span_rows
        return ids + jnp.where(ids < span_rows, first, second)

    q_pos = span_pos(me, (1, rows), 1)
    allowed = []
    for source_of in plan:
        source, valid = source_of(me)
        k_pos = span_pos(source, (rows, 1), 0)
        if valid is not None:
            k_pos = jnp.where(valid, k_pos, jnp.int32(2**30))
        allowed.append(k_pos <= q_pos)
    for h in range(heads):
        cols = slice(h * HEAD_SIZE, (h + 1) * HEAD_SIZE)
        kv_cols = slice(h // group * HEAD_SIZE, (h // group + 1) * HEAD_SIZE)
        if has_state:
            acc = acc_in[cols, :]
            top = stat_in[h : h + 1, :]
            total = stat_in[heads + h : heads + h + 1, :]
        else:
            acc = None
        for (k_ref, v_ref), ok in zip(pieces, allowed):
            scores = lax.dot_general(
                k_ref[:, kv_cols],
                q_ref[:, cols],
                (((1,), (1,)), ((), ())),
                preferred_element_type=jnp.float32,
            )
            masked = jnp.where(ok, scores, MASKED)
            piece_top = jnp.maximum(jnp.max(masked, axis=0, keepdims=True), LOW)
            weights = jnp.exp2((masked - piece_top) * factor)
            piece_total = jnp.sum(weights, axis=0, keepdims=True)
            piece_sum = lax.dot_general(
                v_ref[:, kv_cols],
                weights.astype(jnp.bfloat16),
                (((0,), (0,)), ((), ())),
                preferred_element_type=jnp.float32,
            )
            if acc is None:
                acc, top, total = piece_sum, piece_top, piece_total
            else:
                new_top = jnp.maximum(top, piece_top)
                keep = jnp.exp2((top - new_top) * factor)
                add = jnp.exp2((piece_top - new_top) * factor)
                acc = acc * keep + piece_sum * add
                total = total * keep + piece_total * add
                top = new_top
        if last:
            outs[0][:, cols] = (acc / total).T.astype(jnp.bfloat16)
        else:
            outs[0][cols, :] = acc
            outs[1][h : h + 1, :] = top
            outs[1][heads + h : heads + h + 1, :] = total


def attend(span_order, q, pieces, plan, state, last):
    rows, width = q.shape
    heads = width // HEAD_SIZE
    group = width // pieces[0][0].shape[1]
    vmem = pl.BlockSpec(memory_space=pltpu.VMEM)
    operands = [span_order, q]
    specs = [pl.BlockSpec(memory_space=pltpu.SMEM), vmem]
    for k, v in pieces:
        operands += [k, v]
        specs += [vmem, vmem]
    if state is not None:
        operands += list(state)
        specs += [vmem, vmem]
    if last:
        out_shape = jax.ShapeDtypeStruct((rows, width), jnp.bfloat16)
        out_specs = vmem
    else:
        out_shape = (
            jax.ShapeDtypeStruct((width, rows), jnp.float32),
            jax.ShapeDtypeStruct((2 * heads, rows), jnp.float32),
        )
        out_specs = (vmem, vmem)

    def body(*refs):
        attend_kernel(rows // 2, group, plan, state is not None, last, *refs)

    return pl.pallas_call(
        body,
        out_shape=out_shape,
        in_specs=specs,
        out_specs=out_specs,
        compiler_params=pltpu.CompilerParams(vmem_limit_bytes=24 * 1024 * 1024),
    )(*operands)


def shards_any(queries, keys, values, span_order):
    n = lax.axis_size("ctx")
    rows = queries.shape[0]
    k_all = lax.all_gather(keys, "ctx", axis=0, tiled=True)
    v_all = lax.all_gather(values, "ctx", axis=0, tiled=True)
    state = None
    for s in range(n):
        piece = (k_all[s * rows : (s + 1) * rows], v_all[s * rows : (s + 1) * rows])
        state = attend(span_order, queries, [piece], [lambda me, s=s: (s, None)], state, s == n - 1)
    return state


def shards(queries, keys, values, span_order):
    if lax.axis_size("ctx") != 4:
        return shards_any(queries, keys, values, span_order)

    def send(pairs):
        return [lax.ppermute(x, "ctx", pairs) for x in (keys, values)]

    far = send([(0, 2), (2, 0), (1, 3), (3, 1)])
    near = send([(0, 1), (1, 0), (2, 3), (3, 2)])
    cross = send([(0, 3), (3, 0), (1, 2), (2, 1)])
    state = attend(span_order, queries, [(keys, values)], [lambda me: (me, None)], None, False)
    state = attend(
        span_order, queries, [near], [lambda me: (me + 1 - 2 * (me % 2), None)], state, False
    )
    state = attend(span_order, queries, [far], [lambda me: ((me + 2) % 4, None)], state, False)
    return attend(span_order, queries, [cross], [lambda me: (3 - me, None)], state, True)


def solution(mesh):
    spec = P(("groups", "ctx"), ("head", "rep"))
    return jax.shard_map(
        shards,
        mesh=mesh,
        in_specs=(spec, spec, spec, P()),
        out_specs=spec,
        check_vma=False,
    )
```

time: 61 us -> 31.9 us (0.52)
  blocking collectives: 34.1 us -> 0 us
  Pallas kernels: 0 us -> 12.9 us
  starting transfers between devices: 0 us -> 12.6 us
  matrix products: 8.65 us -> 0 us
  other arithmetic: 7.94 us -> 0 us
  local copies, waits for them, and re-layouts: 9.69 us -> 3.5 us
  waiting for transfers between devices: 0 us -> 2.6 us
    all_gather x2 -> x0, blocking collectives: 34.1 us -> none  [the longest x1 17.6 us: shards(): k_piece = lax.all_gather(keys, 'ctx', axis=0, tiled=True)]
    pallas_call x0 -> x4, Pallas kernels: none -> 12.9 us  [attend(): pl.pallas_call(body, out_shape=out_shape, in_specs=specs, out_specs=out_s...]
    ppermute x0 -> x6, starting transfers between devices: none -> 12.6 us  [send(): return [lax.ppermute(x, 'ctx', pairs) for x in (keys, values)]]
    dot_general x4 -> x0, matrix products: 8.65 us -> none  [the longest x2 4.85 us: source_partials(): jnp.einsum('crhgs,cshd->crhgd', weights.astype(jnp.bfloat16), value_group...]
    dynamic_slice x4 -> x0, local copies, waits for them, and re-layouts: 4.53 us -> none  [shards(): running, unused = lax.scan(one_turn, running, (k_steps, v_steps, p_steps))]
    add x6 -> x0, other arithmetic: 4.32 us -> none  [the longest x2 4.23 us: absorb(): run_sum * rescale[..., None]]
    ppermute x0 -> x6, waiting for transfers between devices: none -> 2.6 us  [send(): return [lax.ppermute(x, 'ctx', pairs) for x in (keys, values)]]
    convert_element_type x3 -> x0, other arithmetic: 2.44 us -> none  [the longest x2 2.34 us: source_partials(): weights.astype(jnp.bfloat16)]
  transfers between devices with their start and end apart: 0 -> 6, of which waited for: 0 -> 2; matrix products, arithmetic and copies ran while one was open for 0% -> 0% of each run, Pallas kernels for 0% -> 28%
where the time goes in v1:
time: 31.9 us; the launch traced here: 31.7 us
  Pallas kernels  12.9 us (40%)
  starting transfers between devices  12.6 us (39%)
  local copies, waits for them, and re-layouts  3.5 us (11%)
  waiting for transfers between devices  2.6 us (8%)
    pallas_call x4, Pallas kernels, attend(): pl.pallas_call(body, out_shape=out_shape, in_specs=specs, out_specs=out_s...  12.9 us
    ppermute x6, starting transfers between devices, send(): return [lax.ppermute(x, 'ctx', pairs) for x in (keys, values)]  12.6 us
    unnamed x8, local copies, waits for them, and re-layouts  3.5 us
    ppermute x6, waiting for transfers between devices, send(): return [lax.ppermute(x, 'ctx', pairs) for x in (keys, values)]  2.6 us
  transfers between devices with their start and end apart: 6, of which 2 were waited for; matrix products, arithmetic and copies ran while one was open for 0% of the time, Pallas kernels for 28%

profile of v1, /device:TPU:0, one launch (start us, length us, event | category | flops | bytes accessed | tf_op | source)
XLA Modules:
  0.0 31.7 jit_solution(13692158971108029902)
XLA Ops:
  0.0 3.1 %collective-permute-start.4 = (bf16[256,256]{1,0:T(8,128)(2,1)}, bf16[256,256]{1,0:T(8,128)(2,1)S(1)}, u32[]{:S(2)}, u32[]{:S(2)}) collective-permute-start(bf16[256,256]{1,0:T(8,128)(2,1)} %refs_2_.1), channel_id=1, source_target_pairs={{0,4},{4,0},{8,12},{12,8},{1,5},{5,1},{9,13},{13,9},{2,6},{6,2},{1... | collective-permute-start | bytes 393224 | tf_op jit(solution)/shard_map/ppermute | solution.py:140
  3.1 0.0 collective-permute-start.5
  3.1 3.0 %collective-permute-start.2 = (bf16[256,256]{1,0:T(8,128)(2,1)}, bf16[256,256]{1,0:T(8,128)(2,1)S(1)}, u32[]{:S(2)}, u32[]{:S(2)}) collective-permute-start(bf16[256,256]{1,0:T(8,128)(2,1)} %refs_2_.1), channel_id=1, source_target_pairs={{0,8},{8,0},{4,12},{12,4},{1,9},{9,1},{5,13},{13,5},{2,10},{10,2},... | collective-permute-start | bytes 393224 | tf_op jit(solution)/shard_map/ppermute | solution.py:140
  6.1 0.0 collective-permute-start.3
  6.1 3.9 %collective-permute-start = (bf16[256,256]{1,0:T(8,128)(2,1)}, bf16[256,256]{1,0:T(8,128)(2,1)S(1)}, u32[]{:S(2)}, u32[]{:S(2)}) collective-permute-start(bf16[256,256]{1,0:T(8,128)(2,1)} %refs_2_.1), channel_id=1, source_target_pairs={{0,12},{12,0},{4,8},{8,4},{1,13},{13,1},{5,9},{9,5},{2,14},{14,2},... | collective-permute-start | bytes 393224 | tf_op jit(solution)/shard_map/ppermute | solution.py:140
  10.0 2.1 %collective-permute-done.4.refs_2_ = bf16[256,256]{1,0:T(8,128)(2,1)S(1)} collective-permute-done((bf16[256,256]{1,0:T(8,128)(2,1)}, bf16[256,256]{1,0:T(8,128)(2,1)S(1)}, u32[]{:S(2)}, u32[]{:S(2)}) %collective-permute-start.4) | collective-permute-done | bytes 131104 | tf_op jit(solution)/shard_map/ppermute | solution.py:140
  12.2 2.6 %collective-permute-start.1 = (bf16[256,256]{1,0:T(8,128)(2,1)}, bf16[256,256]{1,0:T(8,128)(2,1)S(1)}, u32[]{:S(2)}, u32[]{:S(2)}) collective-permute-start(bf16[256,256]{1,0:T(8,128)(2,1)} %refs_3_.1), channel_id=1, source_target_pairs={{0,12},{12,0},{4,8},{8,4},{1,13},{13,1},{5,9},{9,5},{2,14},{14,2},... | collective-permute-start | bytes 393224 | tf_op jit(solution)/shard_map/ppermute | solution.py:140
  14.7 0.0 copy-start
  14.7 1.0 %copy-done = bf16[256,1024]{1,0:T(8,128)(2,1)S(1)} copy-done((bf16[256,1024]{1,0:T(8,128)(2,1)S(1)}, bf16[256,1024]{1,0:T(8,128)(2,1)}, u32[]{:S(2)}) %copy-start) | copy-done | bytes 524312
  15.8 0.0 copy-start.1
  15.8 0.9 %copy-done.1 = bf16[256,256]{1,0:T(8,128)(2,1)S(1)} copy-done((bf16[256,256]{1,0:T(8,128)(2,1)S(1)}, bf16[256,256]{1,0:T(8,128)(2,1)}, u32[]{:S(2)}) %copy-start.1) | copy-done | bytes 131096
  16.7 0.0 copy-start.2
  16.7 0.9 %copy-done.2 = bf16[256,256]{1,0:T(8,128)(2,1)S(1)} copy-done((bf16[256,256]{1,0:T(8,128)(2,1)S(1)}, bf16[256,256]{1,0:T(8,128)(2,1)}, u32[]{:S(2)}) %copy-start.2) | copy-done | bytes 131096
  17.6 0.0 copy-start.3
  17.6 0.7 %copy-done.3 = s32[8]{0:T(128)S(1)} copy-done((s32[8]{0:T(128)S(1)}, s32[8]{0:T(128)}, u32[]{:S(2)}) %copy-start.3) | copy-done | bytes 56
  18.2 3.0 %shard_map.46 = (f32[1024,256]{1,0:T(8,128)S(1)}, f32[16,256]{1,0:T(8,128)S(1)}) custom-call(s32[8]{0:T(128)S(1)} %copy-done.3, bf16[256,1024]{1,0:T(8,128)(2,1)S(1)} %copy-done, bf16[256,256]{1,0:T(8,128)(2,1)S(1)} %copy-done.1, bf16[256,256]{1,0:T(8,128)(2,1)S(1)} %copy-done.2), custom_call_target="tpu_custom_call" | custom-call | tf_op jit(solution)/shard_map/pallas_call | solution.py:114
  21.2 0.0 collective-permute-done.5.refs_3_
  21.3 3.0 %shard_map.47 = (f32[1024,256]{1,0:T(8,128)S(1)}, f32[16,256]{1,0:T(8,128)S(1)}) custom-call(s32[8]{0:T(128)S(1)} %copy-done.3, bf16[256,1024]{1,0:T(8,128)(2,1)S(1)} %copy-done, bf16[256,256]{1,0:T(8,128)(2,1)S(1)} %collective-permute-done.4.refs_2_, bf16[256,256]{1,0:T(8,128)(2,1)S(1)} %collective-permute-done.5.refs_3_, ...), custom_call_target="tpu_custom_call" | custom-call | tf_op jit(solution)/shard_map/pallas_call | solution.py:114
  24.3 0.0 collective-permute-done.2.refs_2_
  24.3 0.4 %collective-permute-done.3.refs_3_ = bf16[256,256]{1,0:T(8,128)(2,1)S(1)} collective-permute-done((bf16[256,256]{1,0:T(8,128)(2,1)}, bf16[256,256]{1,0:T(8,128)(2,1)S(1)}, u32[]{:S(2)}, u32[]{:S(2)}) %collective-permute-start.3) | collective-permute-done | bytes 131104 | tf_op jit(solution)/shard_map/ppermute | solution.py:140
  24.7 3.0 %shard_map.48 = (f32[1024,256]{1,0:T(8,128)S(1)}, f32[16,256]{1,0:T(8,128)S(1)}) custom-call(s32[8]{0:T(128)S(1)} %copy-done.3, bf16[256,1024]{1,0:T(8,128)(2,1)S(1)} %copy-done, bf16[256,256]{1,0:T(8,128)(2,1)S(1)} %collective-permute-done.2.refs_2_, bf16[256,256]{1,0:T(8,128)(2,1)S(1)} %collective-permute-done.3.refs_3_, ...), custom_call_target="tpu_custom_call" | custom-call | tf_op jit(solution)/shard_map/pallas_call | solution.py:114
  27.8 0.0 collective-permute-done.refs_2_
  27.8 0.0 collective-permute-done.1.refs_3_
  27.8 3.9 %shard_map.49 = bf16[256,1024]{1,0:T(8,128)(2,1)} custom-call(s32[8]{0:T(128)S(1)} %copy-done.3, bf16[256,1024]{1,0:T(8,128)(2,1)S(1)} %copy-done, bf16[256,256]{1,0:T(8,128)(2,1)S(1)} %collective-permute-done.refs_2_, bf16[256,256]{1,0:T(8,128)(2,1)S(1)} %collective-permute-done.1.refs_3_, f32[1024,256]{1,0:T(8,128)S(1)} %get-tuple-element.15.refs_4_, ...), custom_call_target="tpu_custom_call" | custom-call | tf_op jit(solution)/shard_map/pallas_call | solution.py:114
Async XLA Ops:
  0.0 12.2 %collective-permute-start.4 = (bf16[256,256]{1,0:T(8,128)(2,1)}, bf16[256,256]{1,0:T(8,128)(2,1)S(1)}, u32[]{:S(2)}, u32[]{:S(2)}) collective-permute-start(bf16[256,256]{1,0:T(8,128)(2,1)} %refs_2_.1), channel_id=1, source_target_pairs={{0,4},{4,0},{8,12},{12,8},{1,5},{5,1},{9,13},{13,9},{2,6},{6,2},{1... | collective-permute-start | bytes 393224 | tf_op jit(solution)/shard_map/ppermute | solution.py:140
  3.1 18.2 %collective-permute-start.5 = (bf16[256,256]{1,0:T(8,128)(2,1)}, bf16[256,256]{1,0:T(8,128)(2,1)S(1)}, u32[]{:S(2)}, u32[]{:S(2)}) collective-permute-start(bf16[256,256]{1,0:T(8,128)(2,1)} %refs_3_.1), channel_id=1, source_target_pairs={{0,4},{4,0},{8,12},{12,8},{1,5},{5,1},{9,13},{13,9},{2,6},{6,2},{1... | collective-permute-start | bytes 393224 | tf_op jit(solution)/shard_map/ppermute | solution.py:140
  3.1 21.2 %collective-permute-start.2 = (bf16[256,256]{1,0:T(8,128)(2,1)}, bf16[256,256]{1,0:T(8,128)(2,1)S(1)}, u32[]{:S(2)}, u32[]{:S(2)}) collective-permute-start(bf16[256,256]{1,0:T(8,128)(2,1)} %refs_2_.1), channel_id=1, source_target_pairs={{0,8},{8,0},{4,12},{12,4},{1,9},{9,1},{5,13},{13,5},{2,10},{10,2},... | collective-permute-start | bytes 393224 | tf_op jit(solution)/shard_map/ppermute | solution.py:140
  6.1 18.6 %collective-permute-start.3 = (bf16[256,256]{1,0:T(8,128)(2,1)}, bf16[256,256]{1,0:T(8,128)(2,1)S(1)}, u32[]{:S(2)}, u32[]{:S(2)}) collective-permute-start(bf16[256,256]{1,0:T(8,128)(2,1)} %refs_3_.1), channel_id=1, source_target_pairs={{0,8},{8,0},{4,12},{12,4},{1,9},{9,1},{5,13},{13,5},{2,10},{10,2},... | collective-permute-start | bytes 393224 | tf_op jit(solution)/shard_map/ppermute | solution.py:140
  6.1 21.6 %collective-permute-start = (bf16[256,256]{1,0:T(8,128)(2,1)}, bf16[256,256]{1,0:T(8,128)(2,1)S(1)}, u32[]{:S(2)}, u32[]{:S(2)}) collective-permute-start(bf16[256,256]{1,0:T(8,128)(2,1)} %refs_2_.1), channel_id=1, source_target_pairs={{0,12},{12,0},{4,8},{8,4},{1,13},{13,1},{5,9},{9,5},{2,14},{14,2},... | collective-permute-start | bytes 393224 | tf_op jit(solution)/shard_map/ppermute | solution.py:140
  12.2 15.6 %collective-permute-start.1 = (bf16[256,256]{1,0:T(8,128)(2,1)}, bf16[256,256]{1,0:T(8,128)(2,1)S(1)}, u32[]{:S(2)}, u32[]{:S(2)}) collective-permute-start(bf16[256,256]{1,0:T(8,128)(2,1)} %refs_3_.1), channel_id=1, source_target_pairs={{0,12},{12,0},{4,8},{8,4},{1,13},{13,1},{5,9},{9,5},{2,14},{14,2},... | collective-permute-start | bytes 393224 | tf_op jit(solution)/shard_map/ppermute | solution.py:140
  14.7 1.0 %copy-start = (bf16[256,1024]{1,0:T(8,128)(2,1)S(1)}, bf16[256,1024]{1,0:T(8,128)(2,1)}, u32[]{:S(2)}) copy-start(bf16[256,1024]{1,0:T(8,128)(2,1)} %refs_1_.7) | copy-start | bytes 1572868
  15.8 0.9 %copy-start.1 = (bf16[256,256]{1,0:T(8,128)(2,1)S(1)}, bf16[256,256]{1,0:T(8,128)(2,1)}, u32[]{:S(2)}) copy-start(bf16[256,256]{1,0:T(8,128)(2,1)} %refs_2_.1) | copy-start | bytes 393220
  16.7 0.9 %copy-start.2 = (bf16[256,256]{1,0:T(8,128)(2,1)S(1)}, bf16[256,256]{1,0:T(8,128)(2,1)}, u32[]{:S(2)}) copy-start(bf16[256,256]{1,0:T(8,128)(2,1)} %refs_3_.1) | copy-start | bytes 393220
  17.6 0.7 %copy-start.3 = (s32[8]{0:T(128)S(1)}, s32[8]{0:T(128)}, u32[]{:S(2)}) copy-start(s32[8]{0:T(128)} %refs_0_.7) | copy-start | bytes 100
